TPU v7x, 32 devices: a whole 2x2x4 slice. The times are simulated.
32 devices in a mesh: groups: 2 (over y), seq: 4 (over z), head: 2 (over x), inner: 2 (over core).
Axes of the slice: x: 2, y: 2, z: 4, core: 2. Of those that a mesh axis runs over, the one named last changes fastest.
Arguments:
- queries: bfloat16 [4096, 2, 8, 128], P(('groups', 'seq'), 'head', 'inner'), parts along dimension 0, may hold values from -120 to 120
- grad_out: bfloat16 [4096, 2, 8, 128], P(('groups', 'seq'), 'head', 'inner'), parts along dimension 0, may hold values from -6 to 6
- keys: bfloat16 [4096, 2, 128], P(('groups', 'seq'), 'head'), parts along dimension 0, may hold values from -6 to 6
- values: bfloat16 [4096, 2, 128], P(('groups', 'seq'), 'head'), parts along dimension 0, may hold values from -6 to 6
- indices: int32 [2, 64, 16], P('head', 'groups'), parts along dimension 1, may hold values from 0 to 31, as said below
- valid: int32 [2, 64, 16], P('head', 'groups'), parts along dimension 1, may hold values from 0 to 1
Outputs:
- grad_queries: bfloat16 [4096, 2, 8, 128], P(('groups', 'seq'), 'head', 'inner'), parts along dimension 0
- grad_keys: bfloat16 [4096, 2, 128], P(('groups', 'seq'), 'head'), parts along dimension 0
- grad_values: bfloat16 [4096, 2, 128], P(('groups', 'seq'), 'head'), parts along dimension 0
There are 2 independent parts, one for each index of `groups`. A program takes and returns all parts, laid end to end along the dimension named above; each array names one. Nothing has to cross between parts.
Inputs may be any that keep to these rules, and one draw needn't show every extreme that they name: `indices`: call blocks r * 8 to r * 8 + 7 run r. For every KV head and query block b: slot 0 names b and is valid; the valid slots name distinct blocks at most b; over all query blocks of run r, the valid slots name blocks of runs later than r never, and for each earlier run exactly 4 distinct blocks of it. Slots that are not valid name arbitrary blocks.
All inputs are finite; a program needn't handle non-finite values.
Results may differ from a plain program's by a relative error of at most 0.007.
Values may be sent and summed in bfloat16 or wider, within the bound.
A program may use at most 64 MiB of HBM per device.

v0:
```python
import functools
import math

import jax
import jax.numpy as jnp
from jax import lax
from jax.experimental import pallas as pl
from jax.experimental.pallas import tpu as pltpu
from jax.sharding import PartitionSpec as P

BLK = 64
CAP = 4
MESH = pl.DeviceIdType.MESH
NEG = -1e30
NT = (((1,), (1,)), ((), ()))
F32 = jnp.float32
BF = jnp.bfloat16


def dot(a, b):
    return jnp.dot(a, b, preferred_element_type=F32)


def dot_nt(a, b):
    return lax.dot_general(a, b, NT, preferred_element_type=F32)


def log2(n):
    shift = n.bit_length() - 1
    assert 1 << shift == n
    return shift


def iota(shape, axis):
    return lax.broadcasted_iota(jnp.int32, shape, axis)


def kernel(
    cfg,
    q_ref, do_ref, k_ref, v_ref, idx_ref, val_ref,
    dq_ref, dk_ref, dv_ref,
    sel, qaug, qd, kv, oh, kt, stage, pool, wt,
    s_own, dp_own, s_rem, dp_rem, pd, xsend, xrecv, tsend, trecv, ox_send, ox_recv, acc,
    a_send, a_recv, f_send, f_recv, x_send, x_recv, t_send, t_recv, o_sem, r_sem, in_sem, dq_buf, stats,
):
    S, heads, nb, total, topk, width, supers, pre, nbuf = cfg
    me = lax.axis_index("seq")
    core = lax.axis_index("inner")
    mate = 1 - core
    chunk = CAP * BLK
    nrem = (S - 1) * chunk
    rows_b = BLK * heads
    own_rows = nb * BLK
    lanes = sel.shape[1]
    slot_lanes = oh.shape[1]
    scaling = 1.0 / math.sqrt(width)
    c2 = scaling * math.log2(math.e)

    barrier = pltpu.get_barrier_semaphore()

    def hello(j, _):
        pl.semaphore_signal(
            barrier, inc=1, device_id={"seq": lax.rem(me + 1 + j, S)}, device_id_type=MESH
        )
        return 0

    lax.fori_loop(0, S - 1, hello, 0)
    pl.semaphore_signal(barrier, inc=1, device_id={"inner": mate}, device_id_type=MESH)

    loads = [
        pltpu.make_async_copy(src, dst, in_sem.at[i])
        for i, (src, dst) in enumerate(
            ((k_ref, kv.at[0]), (v_ref, kv.at[1]), (q_ref, qd.at[0]), (do_ref, qd.at[1]))
        )
    ]
    for load in loads:
        load.start()
    picked = jnp.where(val_ref[...] > 0, idx_ref[...], -1)
    block = iota((lanes, total), 0)
    hit = jnp.zeros((lanes, total), F32)
    for t in range(topk):
        hit = jnp.where(picked[t : t + 1, :] == block, 1.0, hit)
    eye = jnp.where(iota((total, total), 0) == iota((total, total), 1), 1.0, 0.0).astype(BF)
    sel[...] = dot_nt(eye, hit.astype(BF))
    nb_shift = log2(nb)
    tri_r = iota((lanes, lanes), 0)
    tri_c = iota((lanes, lanes), 1)
    tri = jnp.where(
        (tri_r < tri_c)
        & (lax.shift_right_logical(tri_r, nb_shift) == lax.shift_right_logical(tri_c, nb_shift)),
        1.0,
        0.0,
    ).astype(BF)

    def ranks(run):
        rows = sel[pl.ds(pl.multiple_of(run * nb, nb), nb), :]
        present = jnp.max(rows, axis=0, keepdims=True)
        rank = dot(jnp.broadcast_to(present, (8, lanes)).astype(BF), tri)[0:1, :]
        return rows, present, rank

    loads[0].wait()
    loads[1].wait()
    pl.semaphore_wait(barrier, S)

    def expand(axis):
        shape = (lanes, own_rows) if axis else (own_rows, lanes)
        block = lax.shift_right_logical(iota(shape, axis), log2(BLK)) + me * nb
        return jnp.where(block == iota(shape, 1 - axis), 1.0, 0.0).astype(BF)

    spread = expand(1)
    spread_t = expand(0)

    def send_a(r):
        return pltpu.make_async_remote_copy(
            src_ref=stage.at[r],
            dst_ref=pool.at[core, pl.ds(pl.multiple_of(me * chunk, chunk), chunk)],
            send_sem=a_send.at[r],
            recv_sem=a_recv.at[me],
            device_id={"seq": r},
            device_id_type=MESH,
        )

    def code_of(r):
        _, present, rank = ranks(r)
        return jnp.broadcast_to(jnp.where(present > 0.5, rank, -8.0), (8, lanes)).astype(BF)

    def scatter_of(code):
        down = dot_nt(spread_t, jnp.broadcast_to(code[0:1, :], (chunk, lanes)))
        down = down.astype(jnp.int32) * BLK + (iota((own_rows, chunk), 0) & (BLK - 1))
        return jnp.where(down == iota((own_rows, chunk), 1), 1.0, 0.0).astype(BF)

    def give(j, _):
        r = S - 1 - j
        code = code_of(r)
        across = dot(code, spread)[0:1, :].astype(jnp.int32) * BLK
        across = across + (iota((1, own_rows), 1) & (BLK - 1))
        pick = jnp.where(across == iota((chunk, own_rows), 0), 1.0, 0.0).astype(BF)
        stage[r] = dot(pick, kv[core]).astype(BF)
        send_a(r).start()
        if pre:
            wt[r] = scatter_of(code)
        return 0

    lax.fori_loop(0, S - 1 - me, give, 0)

    mine, present, rank = ranks(me)
    block_row = iota((1, lanes), 1)
    run_row = lax.shift_right_logical(block_row, nb_shift)
    place = jnp.where(
        run_row < me,
        run_row * CAP + rank.astype(jnp.int32),
        (S - 1) * CAP + (block_row & (nb - 1)),
    )
    place = jnp.where((present > 0.5) & (run_row <= me), place, -1)
    table = jnp.where(place == iota((slot_lanes, lanes), 0), 1.0, 0.0).astype(BF)
    bias = jnp.where(dot_nt(mine.astype(BF), table) > 0.5, 0.0, NEG)
    loads[2].wait()
    loads[3].wait()
    for b in range(nb):
        rows = pl.ds(b * rows_b, rows_b)
        qaug[rows, 0:width] = qd[0, rows, :]
        qaug[rows, width:] = jnp.broadcast_to(bias[b : b + 1, :], (rows_b, slot_lanes)).astype(BF)
    nkeys = oh.shape[0]
    oh[...] = jnp.where(
        lax.shift_right_logical(iota((nkeys, slot_lanes), 0), log2(BLK))
        == iota((nkeys, slot_lanes), 1),
        1.0,
        0.0,
    ).astype(BF)
    kt[:, nrem:] = kv[0].astype(F32).T.astype(BF)

    pair = 2 if nb % 2 == 0 else 1

    def own_count(b):
        return (b // pair + 1) * pair * BLK

    def own_scores(b, at):
        n = own_count(b)
        rows = pl.ds(b * rows_b, rows_b)
        ka = jnp.concatenate([kv[0, 0:n, :], oh[nrem : nrem + n, :]], axis=1)
        s = dot_nt(ka, qaug[rows, :])
        key = iota((n, rows_b), 0) - b * BLK
        query = lax.shift_right_logical(iota((n, rows_b), 1), log2(heads))
        s_own[at, 0:n, :] = jnp.where(key > query, NEG, s)
        dp_own[at, 0:n, :] = dot_nt(kv[1, 0:n, :], qd[1, rows, :])

    def fold(x, how):
        return how(x.reshape(-1, 8, rows_b), axis=0)

    if pre:
        for b in range(nb):
            own_scores(b, b)

    def blank(s, _):
        at = pl.ds(pl.multiple_of(s * chunk, chunk), chunk)
        pool[0, at, :] = jnp.zeros((chunk, width), BF)
        pool[1, at, :] = jnp.zeros((chunk, width), BF)
        return 0

    lax.fori_loop(me, S - 1, blank, 0)

    def pool_at(kind, s):
        return pool.at[kind, pl.ds(pl.multiple_of(s * chunk, chunk), chunk)]

    def recv_a(s):
        return pltpu.make_async_remote_copy(
            src_ref=stage.at[s],
            dst_ref=pool_at(core, s),
            send_sem=a_send.at[s],
            recv_sem=a_recv.at[s],
            device_id={"seq": s},
            device_id_type=MESH,
        )

    def forward(kind, s):
        return pltpu.make_async_remote_copy(
            src_ref=pool_at(kind, s),
            dst_ref=pool_at(kind, s),
            send_sem=f_send.at[s],
            recv_sem=f_recv.at[s],
            device_id={"inner": mate},
            device_id_type=MESH,
        )

    def pass_on(j, _):
        s = me - 1 - j
        recv_a(s).wait_recv()
        forward(core, s).start()
        return 0

    lax.fori_loop(0, me, pass_on, 0)

    def take(j, _):
        s = me - 1 - j
        forward(mate, s).wait_recv()
        return 0

    lax.fori_loop(0, me, take, 0)

    step = nrem // supers

    def loop(body, init):
        for j in range(supers):
            init = body(j, init)
        return init

    def span(j):
        return pl.ds(j * step, step)

    for s in range(S - 1):
        kt[:, s * chunk : (s + 1) * chunk] = (
            pool[0, s * chunk : (s + 1) * chunk, :].astype(F32).T.astype(BF)
        )

    def third_on(s_view, dp_view, where, rows, keys_at, inv, delta):
        p = s_view[where] * inv
        pd[1, keys_at, rows] = p.astype(BF)
        pd[0, keys_at, rows] = (p * (dp_view[where] - delta)).astype(BF)

    for b in range(nb):
        at = b if pre else 0
        buf = b % nbuf
        n = own_count(b)
        rows = pl.ds(b * rows_b, rows_b)
        if not pre:
            own_scores(b, 0)
        qa = qaug[rows, :]
        dob = qd[1, rows, :]

        def first(j, m):
            here = span(j)
            ka = jnp.concatenate([pool[0, here, :], oh[here, :]], axis=1)
            s = dot_nt(ka, qa)
            s_rem[buf, here, :] = s
            dp_rem[buf, here, :] = dot_nt(pool[1, here, :], dob)
            return jnp.maximum(m, fold(s, jnp.max))

        m = loop(first, fold(s_own[at, 0:n, :], jnp.max))
        m = jnp.max(m, axis=0, keepdims=True)

        def second_on(s_view, dp_view, where, carry):
            l, d = carry
            e = jnp.exp2((s_view[where] - m) * c2)
            s_view[where] = e
            return (
                l + fold(e, jnp.sum),
                d + fold(e * dp_view[where], jnp.sum),
            )

        zero = jnp.zeros((8, rows_b), F32)
        carry = second_on(s_own, dp_own, (at, slice(0, n)), (zero, zero))
        l, d = loop(lambda j, c: second_on(s_rem, dp_rem, (buf, span(j)), c), carry)
        inv = 1.0 / jnp.sum(l, axis=0, keepdims=True)
        delta = jnp.sum(d, axis=0, keepdims=True) * inv

        if pre:
            stats[b, 0:1, :] = inv
            stats[b, 1:2, :] = delta
        else:
            third_on(s_own, dp_own, (at, slice(0, n)), rows, pl.ds(nrem, n), inv, delta)

        def third(j, c):
            third_on(s_rem, dp_rem, (buf, span(j)), rows, span(j), inv, delta)
            return c

        loop(third, 0)

    def scale_of(kind):
        return jnp.where(kind == 0, scaling, 1.0).astype(F32)

    def remote_terms(kind, s):
        at = pl.ds(pl.multiple_of(s * chunk, chunk), chunk)
        return dot(pd[kind, at, :], qd[kind]) * scale_of(kind)

    def swap(s):
        return pltpu.make_async_remote_copy(
            src_ref=xsend.at[s],
            dst_ref=xrecv.at[s],
            send_sem=x_send.at[s],
            recv_sem=x_recv.at[s],
            device_id={"inner": mate},
            device_id_type=MESH,
        )

    def give_back(s):
        return pltpu.make_async_remote_copy(
            src_ref=tsend.at[s],
            dst_ref=trecv.at[me],
            send_sem=t_send.at[s],
            recv_sem=t_recv.at[me],
            device_id={"seq": s},
            device_id_type=MESH,
        )

    def other(s, _):
        xsend[s] = remote_terms(mate, s)
        swap(s).start()
        return 0

    lax.fori_loop(0, jnp.minimum(me, 1), other, 0)

    def ours(s, _):
        @pl.when(s + 1 < me)
        def _():
            other(s + 1, 0)

        total_terms = remote_terms(core, s)
        swap(s).wait_recv()
        tsend[s] = (total_terms + xrecv[s]).astype(BF)
        give_back(s).start()
        return 0

    lax.fori_loop(0, me, ours, 0)

    own_swap = pltpu.make_async_remote_copy(
        src_ref=ox_send,
        dst_ref=ox_recv,
        send_sem=o_sem.at[0],
        recv_sem=o_sem.at[1],
        device_id={"inner": mate},
        device_id_type=MESH,
    )

    def own_terms(kind, target):
        for c in range(0, nb, pair):
            n = pair * BLK
            lo = c * rows_b
            target[c * BLK : c * BLK + n, :] = (
                dot(pd[kind, nrem + c * BLK : nrem + c * BLK + n, lo:], qd[kind, lo:, :])
                * scale_of(kind)
            )

    if pre:
        for b in range(nb):
            n = own_count(b)
            third_on(
                s_own, dp_own, (b, slice(0, n)), pl.ds(b * rows_b, rows_b), pl.ds(nrem, n),
                stats[b, 0:1, :], stats[b, 1:2, :],
            )
    own_terms(mate, ox_send)
    own_swap.start()
    own_terms(core, acc)

    for b in range(nb):
        rows = pl.ds(b * rows_b, rows_b)
        n = nrem + own_count(b)
        turned = dot(kt[:, 0:n], pd[0, 0:n, rows]) * scaling
        dq_buf[rows, :] = turned.T.astype(BF)
    store = pltpu.make_async_copy(dq_buf, dq_ref, in_sem.at[4])
    store.start()

    own_swap.wait_recv()
    acc[...] += ox_recv[...]

    def gather(j, _):
        r = me + 1 + j
        pltpu.make_async_remote_copy(
            src_ref=tsend.at[r],
            dst_ref=trecv.at[r],
            send_sem=t_send.at[r],
            recv_sem=t_recv.at[r],
            device_id={"seq": r},
            device_id_type=MESH,
        ).wait_recv()
        acc[...] += dot(wt[r] if pre else scatter_of(code_of(r)), trecv[r])
        return 0

    lax.fori_loop(0, S - 1 - me, gather, 0)

    def last(ref):
        return pltpu.make_async_remote_copy(
            src_ref=ref,
            dst_ref=ref,
            send_sem=r_sem.at[0],
            recv_sem=r_sem.at[1],
            device_id={"inner": mate},
            device_id_type=MESH,
        )

    @pl.when(core == 0)
    def _():
        dk_ref[...] = acc[...].astype(BF)
        last(dk_ref).start()

    @pl.when(core == 1)
    def _():
        dv_ref[...] = acc[...].astype(BF)
        last(dv_ref).start()

    def close_up(j, _):
        send_a(me + 1 + j).wait_send()
        return 0

    lax.fori_loop(0, S - 1 - me, close_up, 0)

    def close_down(s, _):
        forward(core, s).wait_send()
        swap(s).wait_send()
        give_back(s).wait_send()
        return 0

    lax.fori_loop(0, me, close_down, 0)
    own_swap.wait_send()
    store.wait()

    @pl.when(core == 0)
    def _():
        last(dk_ref).wait_send()
        last(dv_ref).wait_recv()

    @pl.when(core == 1)
    def _():
        last(dv_ref).wait_send()
        last(dk_ref).wait_recv()


def per_device(queries, grad_out, keys, values, indices, valid):
    tokens, _, heads, width = queries.shape
    S = lax.axis_size("seq")
    total, topk = indices.shape[1:]
    nb = tokens // BLK
    chunk = CAP * BLK
    nrem = (S - 1) * chunk
    own_rows = tokens
    nkeys = nrem + own_rows
    rows = tokens * heads
    rows_b = BLK * heads
    lanes = -(-total // 128) * 128
    slot_lanes = -(-(nkeys // BLK) // 128) * 128
    supers = next(n for n in range(1, S) if (S - 1) % n == 0 and (S - 1) // n <= 4)
    pre = supers == 1
    nbuf = 2 if pre else 1
    n_own = nb if pre else 1
    cfg = (S, heads, nb, total, topk, width, supers, pre, nbuf)
    vmem = pl.BlockSpec(memory_space=pltpu.VMEM)
    hbm = pl.BlockSpec(memory_space=pl.ANY)
    dma = pltpu.SemaphoreType.DMA
    dq, dk, dv = pl.pallas_call(
        functools.partial(kernel, cfg),
        out_shape=(
            jax.ShapeDtypeStruct((rows, width), BF),
            jax.ShapeDtypeStruct((own_rows, width), BF),
            jax.ShapeDtypeStruct((own_rows, width), BF),
        ),
        in_specs=[hbm] * 4 + [vmem] * 2,
        out_specs=(hbm, vmem, vmem),
        scratch_shapes=[
            pltpu.VMEM((total, lanes), F32),
            pltpu.VMEM((rows, width + slot_lanes), BF),
            pltpu.VMEM((2, rows, width), BF),
            pltpu.VMEM((2, own_rows, width), BF),
            pltpu.VMEM((nkeys, slot_lanes), BF),
            pltpu.VMEM((width, nkeys), BF),
            pltpu.VMEM((S, chunk, width), BF),
            pltpu.VMEM((2, nrem, width), BF),
            pltpu.VMEM((S if pre else 1, own_rows, chunk), BF),
            pltpu.VMEM((n_own, own_rows, rows_b), F32),
            pltpu.VMEM((n_own, own_rows, rows_b), F32),
            pltpu.VMEM((nbuf, nrem, rows_b), F32),
            pltpu.VMEM((nbuf, nrem, rows_b), F32),
            pltpu.VMEM((2, nkeys, rows), BF),
            pltpu.VMEM((S, chunk, width), F32),
            pltpu.VMEM((S, chunk, width), F32),
            pltpu.VMEM((S, chunk, width), BF),
            pltpu.VMEM((S, chunk, width), BF),
            pltpu.VMEM((own_rows, width), F32),
            pltpu.VMEM((own_rows, width), F32),
            pltpu.VMEM((own_rows, width), F32),
            dma((S,)), dma((S,)), dma((S,)), dma((S,)), dma((S,)), dma((S,)),
            dma((S,)), dma((S,)), dma((2,)), dma((2,)),
            dma((5,)),
            pltpu.VMEM((rows, width), BF),
            pltpu.VMEM((nb, 2, rows_b), F32),
        ],
        compiler_params=pltpu.CompilerParams(
            collective_id=0, has_side_effects=True, vmem_limit_bytes=67043328
        ),
    )(
        queries.reshape(rows, width),
        grad_out.reshape(rows, width),
        keys.reshape(own_rows, width),
        values.reshape(own_rows, width),
        indices[0].T,
        valid[0].T,
    )
    return (
        dq.reshape(tokens, 1, heads, width),
        dk.reshape(tokens, 1, width),
        dv.reshape(tokens, 1, width),
    )


def solution(mesh):
    return jax.shard_map(
        per_device,
        mesh=mesh,
        in_specs=(
            P(("groups", "seq"), "head", "inner", None),
            P(("groups", "seq"), "head", "inner", None),
            P(("groups", "seq"), "head", None),
            P(("groups", "seq"), "head", None),
            P("head", "groups", None),
            P("head", "groups", None),
        ),
        out_specs=(
            P(("groups", "seq"), "head", "inner", None),
            P(("groups", "seq"), "head", None),
            P(("groups", "seq"), "head", None),
        ),
        check_vma=False,
    )
```

profile of v0, /device:TPU:0, one launch (start us, length us, event | category | flops | bytes accessed | tf_op | source)
XLA Modules:
  0.0 35.1 jit_solution(15677709733224827421)
XLA Ops:
  0.6 30.8 %shard_map.85 = (bf16[2048,128]{1,0:T(8,128)(2,1)}, bf16[512,128]{1,0:T(8,128)(2,1)}, bf16[512,128]{1,0:T(8,128)(2,1)}) custom-call(bf16[2048,128]{1,0:T(8,128)(2,1)} %bitcast.16, bf16[2048,128]{1,0:T(8,128)(2,1)} %bitcast.17, bf16[512,128]{1,0:T(8,128)(2,1)} %bitcast.20, bf16[512,128]{1,0:T(8,128)(2,1)} %bitcast.21, s32[16,32]{1,0:T(8,128)} %bitcast.22, ...), custom_call_target="tpu_custom_call" | custom-call | tf_op jit(solution)/shard_map/pallas_call | solution.py:478
  31.4 0.0 copy-start.1
  31.5 2.1 %copy.13 = bf16[512,1,4,128]{3,2,1,0:T(4,128)(2,1)} copy(bf16[512,1,4,128]{3,2,1,0:T(4,128)(2,1)} %bitcast.15) | data formatting | bytes 1048576
  33.5 0.0 copy-done.1
  33.5 0.0 copy-start
  33.5 0.7 %copy.14 = bf16[512,1,128]{2,0,1:T(8,128)(2,1)} copy(bf16[512,1,128]{2,0,1:T(8,128)(2,1)S(1)} %bitcast.19) | data formatting | bytes 262144
  34.2 0.3 copy-done
  34.5 0.7 %copy.15 = bf16[512,1,128]{2,0,1:T(8,128)(2,1)} copy(bf16[512,1,128]{2,0,1:T(8,128)(2,1)S(1)} %bitcast.18) | data formatting | bytes 262144
Async XLA Ops:
  31.4 2.1 %copy-start.1 = (bf16[512,128]{1,0:T(8,128)(2,1)S(1)}, bf16[512,128]{1,0:T(8,128)(2,1)}, u32[]{:S(2)}) copy-start(bf16[512,128]{1,0:T(8,128)(2,1)} %get-tuple-element.7) | copy-start | bytes 393220
  33.5 1.0 %copy-start = (bf16[512,128]{1,0:T(8,128)(2,1)S(1)}, bf16[512,128]{1,0:T(8,128)(2,1)}, u32[]{:S(2)}) copy-start(bf16[512,128]{1,0:T(8,128)(2,1)} %get-tuple-element.8) | copy-start | bytes 393220
where the time goes:
time: 35.4 us; the launch traced here: 35.1 us
  Pallas kernels  30.8 us (87%)
  local copies, waits for them, and re-layouts  3.66 us (10%)
  between operations  0.65 us (2%)
    pallas_call x1, Pallas kernels, per_device(): pl.pallas_call(functools.partial(kernel, cfg), out_shape=(jax.ShapeDtypeS...  30.8 us
    unnamed x7, local copies, waits for them, and re-layouts  3.66 us

commit v1 on v0

--- a/solution.py
+++ b/solution.py
@@ -41,7 +41,7 @@
     dq_ref, dk_ref, dv_ref,
     sel, qaug, qd, kv, oh, kt, stage, pool, wt,
     s_own, dp_own, s_rem, dp_rem, pd, xsend, xrecv, tsend, trecv, ox_send, ox_recv, acc,
-    a_send, a_recv, f_send, f_recv, x_send, x_recv, t_send, t_recv, o_sem, r_sem, in_sem, dq_buf, stats,
+    a_send, a_recv, f_send, f_recv, x_send, x_recv, t_send, t_recv, o_sem, r_sem, in_sem, stats,
 ):
     S, heads, nb, total, topk, width, supers, pre, nbuf = cfg
     me = lax.axis_index("seq")
@@ -385,9 +385,7 @@
         rows = pl.ds(b * rows_b, rows_b)
         n = nrem + own_count(b)
         turned = dot(kt[:, 0:n], pd[0, 0:n, rows]) * scaling
-        dq_buf[rows, :] = turned.T.astype(BF)
-    store = pltpu.make_async_copy(dq_buf, dq_ref, in_sem.at[4])
-    store.start()
+        dq_ref[rows, :] = turned.T.astype(BF)
 
     own_swap.wait_recv()
     acc[...] += ox_recv[...]
@@ -441,7 +439,6 @@
 
     lax.fori_loop(0, me, close_down, 0)
     own_swap.wait_send()
-    store.wait()
 
     @pl.when(core == 0)
     def _():
@@ -452,6 +449,26 @@
     def _():
         last(dv_ref).wait_send()
         last(dk_ref).wait_recv()
+
+
+def place_kernel(*refs):
+    n = len(refs) // 2
+    moves = [pltpu.make_async_copy(refs[i], refs[n + i], refs[-1].at[i]) for i in range(n)]
+    for move in moves:
+        move.start()
+    for move in moves:
+        move.wait()
+
+
+def place(*arrays):
+    return pl.pallas_call(
+        place_kernel,
+        out_shape=tuple(jax.ShapeDtypeStruct(a.shape, a.dtype) for a in arrays),
+        in_specs=[pl.BlockSpec(memory_space=pltpu.VMEM)] * len(arrays),
+        out_specs=(pl.BlockSpec(memory_space=pl.ANY),) * len(arrays),
+        scratch_shapes=[pltpu.SemaphoreType.DMA((len(arrays),))],
+        compiler_params=pltpu.CompilerParams(vmem_limit_bytes=65536),
+    )(*(pltpu.with_memory_space_constraint(a, pltpu.VMEM) for a in arrays))
 
 
 def per_device(queries, grad_out, keys, values, indices, valid):
@@ -478,12 +495,12 @@
     dq, dk, dv = pl.pallas_call(
         functools.partial(kernel, cfg),
         out_shape=(
-            jax.ShapeDtypeStruct((rows, width), BF),
-            jax.ShapeDtypeStruct((own_rows, width), BF),
-            jax.ShapeDtypeStruct((own_rows, width), BF),
+            pltpu.VMEM((rows, width), BF),
+            pltpu.VMEM((own_rows, width), BF),
+            pltpu.VMEM((own_rows, width), BF),
         ),
         in_specs=[hbm] * 4 + [vmem] * 2,
-        out_specs=(hbm, vmem, vmem),
+        out_specs=(vmem, vmem, vmem),
         scratch_shapes=[
             pltpu.VMEM((total, lanes), F32),
             pltpu.VMEM((rows, width + slot_lanes), BF),
@@ -509,11 +526,10 @@
             dma((S,)), dma((S,)), dma((S,)), dma((S,)), dma((S,)), dma((S,)),
             dma((S,)), dma((S,)), dma((2,)), dma((2,)),
             dma((5,)),
-            pltpu.VMEM((rows, width), BF),
             pltpu.VMEM((nb, 2, rows_b), F32),
         ],
         compiler_params=pltpu.CompilerParams(
-            collective_id=0, has_side_effects=True, vmem_limit_bytes=67043328
+            collective_id=0, has_side_effects=True, vmem_limit_bytes=67043328 - 6 * own_rows * width * 2 - 4096
         ),
     )(
         queries.reshape(rows, width),
@@ -523,6 +539,7 @@
         indices[0].T,
         valid[0].T,
     )
+    dq, dk, dv = place(dq, dk, dv)
     return (
         dq.reshape(tokens, 1, heads, width),
         dk.reshape(tokens, 1, width),

time: 35.4 us -> 31.9 us (0.901)
  local copies, waits for them, and re-layouts: 3.66 us -> 0 us
    unnamed x7 -> x0, local copies, waits for them, and re-layouts: 3.66 us -> none
    pallas_call x1 -> x2, Pallas kernels: 30.8 us -> 31 us  [the longest x1 30.1 us: per_device(): pl.pallas_call(functools.partial(kernel, cfg), out_shape=(pltpu.VMEM((row...]
where the time goes in v1:
time: 31.9 us; the launch traced here: 31.7 us
  Pallas kernels  31 us (97%)
  between operations  0.64 us (2%)
    pallas_call x1, Pallas kernels, per_device(): pl.pallas_call(functools.partial(kernel, cfg), out_shape=(pltpu.VMEM((row...  30.1 us
    pallas_call x1, Pallas kernels, place(): pl.pallas_call(place_kernel, out_shape=tuple((jax.ShapeDtypeStruct(a.shap...  0.9 us

profile of v1, /device:TPU:0, one launch (start us, length us, event | category | flops | bytes accessed | tf_op | source)
XLA Modules:
  0.0 31.7 jit_solution(7512891236931626844)
XLA Ops:
  0.6 30.1 %shard_map.85 = (bf16[2048,128]{1,0:T(8,128)(2,1)S(1)}, bf16[512,128]{1,0:T(8,128)(2,1)S(1)}, bf16[512,128]{1,0:T(8,128)(2,1)S(1)}) custom-call(bf16[2048,128]{1,0:T(8,128)(2,1)} %bitcast.15, bf16[2048,128]{1,0:T(8,128)(2,1)} %bitcast.16, bf16[512,128]{1,0:T(8,128)(2,1)} %bitcast.17, bf16[512,128]{1,0:T(8,128)(2,1)} %bitcast.18, s32[16,32]{1,0:T(8,128)} %bitcast.19, ...), custom_call_target="tpu_custom_call" | custom-call | tf_op jit(solution)/shard_map/pallas_call | solution.py:495
  30.8 0.9 %shard_map.86 = (bf16[2048,128]{1,0:T(8,128)(2,1)}, bf16[512,128]{1,0:T(8,128)(2,1)}, bf16[512,128]{1,0:T(8,128)(2,1)}) custom-call(bf16[2048,128]{1,0:T(8,128)(2,1)S(1)} %get-tuple-element.9.refs_0_, bf16[512,128]{1,0:T(8,128)(2,1)S(1)} %get-tuple-element.10.refs_1_, bf16[512,128]{1,0:T(8,128)(2,1)S(1)} %get-tuple-element.11.refs_2_), custom_call_target="tpu_custom_call" | custom-call | tf_op jit(solution)/shard_map/pallas_call | solution.py:464

commit v2 on v1

--- a/solution.py
+++ b/solution.py
@@ -37,11 +37,12 @@
 
 def kernel(
     cfg,
-    q_ref, do_ref, k_ref, v_ref, idx_ref, val_ref,
+    q_ref, do_ref, k_ref, v_ref, idx_hbm, val_hbm,
     dq_ref, dk_ref, dv_ref,
     sel, qaug, qd, kv, oh, kt, stage, pool, wt,
     s_own, dp_own, s_rem, dp_rem, pd, xsend, xrecv, tsend, trecv, ox_send, ox_recv, acc,
     a_send, a_recv, f_send, f_recv, x_send, x_recv, t_send, t_recv, o_sem, r_sem, in_sem, stats,
+    ready, slots,
 ):
     S, heads, nb, total, topk, width, supers, pre, nbuf = cfg
     me = lax.axis_index("seq")
@@ -59,23 +60,35 @@
     barrier = pltpu.get_barrier_semaphore()
 
     def hello(j, _):
-        pl.semaphore_signal(
-            barrier, inc=1, device_id={"seq": lax.rem(me + 1 + j, S)}, device_id_type=MESH
-        )
-        return 0
-
-    lax.fori_loop(0, S - 1, hello, 0)
+        pl.semaphore_signal(barrier, inc=1, device_id={"seq": S - 1 - j}, device_id_type=MESH)
+        return 0
+
+    lax.fori_loop(0, S - 1 - me, hello, 0)
     pl.semaphore_signal(barrier, inc=1, device_id={"inner": mate}, device_id_type=MESH)
 
     loads = [
         pltpu.make_async_copy(src, dst, in_sem.at[i])
         for i, (src, dst) in enumerate(
-            ((k_ref, kv.at[0]), (v_ref, kv.at[1]), (q_ref, qd.at[0]), (do_ref, qd.at[1]))
+            (
+                (idx_hbm, slots.at[0]), (val_hbm, slots.at[1]),
+                (k_ref, kv.at[0]), (v_ref, kv.at[1]), (q_ref, qd.at[0]), (do_ref, qd.at[1]),
+            )
         )
     ]
     for load in loads:
         load.start()
-    picked = jnp.where(val_ref[...] > 0, idx_ref[...], -1)
+
+    pl.semaphore_wait(barrier, me + 1)
+
+    def answer(j, _):
+        pl.semaphore_signal(ready.at[me], inc=1, device_id={"seq": j}, device_id_type=MESH)
+        return 0
+
+    lax.fori_loop(0, me, answer, 0)
+
+    loads[0].wait()
+    loads[1].wait()
+    picked = jnp.where(slots[1] > 0, slots[0], -1)
     block = iota((lanes, total), 0)
     hit = jnp.zeros((lanes, total), F32)
     for t in range(topk):
@@ -98,10 +111,6 @@
         rank = dot(jnp.broadcast_to(present, (8, lanes)).astype(BF), tri)[0:1, :]
         return rows, present, rank
 
-    loads[0].wait()
-    loads[1].wait()
-    pl.semaphore_wait(barrier, S)
-
     def expand(axis):
         shape = (lanes, own_rows) if axis else (own_rows, lanes)
         block = lax.shift_right_logical(iota(shape, axis), log2(BLK)) + me * nb
@@ -129,16 +138,18 @@
         down = down.astype(jnp.int32) * BLK + (iota((own_rows, chunk), 0) & (BLK - 1))
         return jnp.where(down == iota((own_rows, chunk), 1), 1.0, 0.0).astype(BF)
 
+    loads[2].wait()
+    loads[3].wait()
+
     def give(j, _):
-        r = S - 1 - j
+        r = me + 1 + j
         code = code_of(r)
         across = dot(code, spread)[0:1, :].astype(jnp.int32) * BLK
         across = across + (iota((1, own_rows), 1) & (BLK - 1))
         pick = jnp.where(across == iota((chunk, own_rows), 0), 1.0, 0.0).astype(BF)
         stage[r] = dot(pick, kv[core]).astype(BF)
+        pl.semaphore_wait(ready.at[r], 1)
         send_a(r).start()
-        if pre:
-            wt[r] = scatter_of(code)
         return 0
 
     lax.fori_loop(0, S - 1 - me, give, 0)
@@ -154,8 +165,8 @@
     place = jnp.where((present > 0.5) & (run_row <= me), place, -1)
     table = jnp.where(place == iota((slot_lanes, lanes), 0), 1.0, 0.0).astype(BF)
     bias = jnp.where(dot_nt(mine.astype(BF), table) > 0.5, 0.0, NEG)
-    loads[2].wait()
-    loads[3].wait()
+    loads[4].wait()
+    loads[5].wait()
     for b in range(nb):
         rows = pl.ds(b * rows_b, rows_b)
         qaug[rows, 0:width] = qd[0, rows, :]
@@ -190,6 +201,15 @@
     if pre:
         for b in range(nb):
             own_scores(b, b)
+
+    if pre:
+
+        def scatters(j, _):
+            r = me + 1 + j
+            wt[r] = scatter_of(code_of(r))
+            return 0
+
+        lax.fori_loop(0, S - 1 - me, scatters, 0)
 
     def blank(s, _):
         at = pl.ds(pl.multiple_of(s * chunk, chunk), chunk)
@@ -499,7 +519,7 @@
             pltpu.VMEM((own_rows, width), BF),
             pltpu.VMEM((own_rows, width), BF),
         ),
-        in_specs=[hbm] * 4 + [vmem] * 2,
+        in_specs=[hbm] * 6,
         out_specs=(vmem, vmem, vmem),
         scratch_shapes=[
             pltpu.VMEM((total, lanes), F32),
@@ -525,8 +545,10 @@
             pltpu.VMEM((own_rows, width), F32),
             dma((S,)), dma((S,)), dma((S,)), dma((S,)), dma((S,)), dma((S,)),
             dma((S,)), dma((S,)), dma((2,)), dma((2,)),
-            dma((5,)),
+            dma((6,)),
             pltpu.VMEM((nb, 2, rows_b), F32),
+            pltpu.SemaphoreType.REGULAR((S,)),
+            pltpu.VMEM((2, topk, total), jnp.int32),
         ],
         compiler_params=pltpu.CompilerParams(
             collective_id=0, has_side_effects=True, vmem_limit_bytes=67043328 - 6 * own_rows * width * 2 - 4096

time: 31.9 us -> 29.9 us (0.937)
  Pallas kernels: 31 us -> 29.1 us
    pallas_call x1, Pallas kernels: 30.1 us -> 28.2 us  [per_device(): pl.pallas_call(functools.partial(kernel, cfg), out_shape=(pltpu.VMEM((row...]
where the time goes in v2:
time: 29.9 us; the launch traced here: 29.7 us
  Pallas kernels  29.1 us (97%)
  between operations  0.64 us (2%)
    pallas_call x1, Pallas kernels, per_device(): pl.pallas_call(functools.partial(kernel, cfg), out_shape=(pltpu.VMEM((row...  28.2 us
    pallas_call x1, Pallas kernels, place(): pl.pallas_call(place_kernel, out_shape=tuple((jax.ShapeDtypeStruct(a.shap...  0.9 us

profile of v2, /device:TPU:0, one launch (start us, length us, event | category | flops | bytes accessed | tf_op | source)
XLA Modules:
  0.0 29.7 jit_solution(14693498760855670207)
XLA Ops:
  0.6 28.2 %shard_map.85 = (bf16[2048,128]{1,0:T(8,128)(2,1)S(1)}, bf16[512,128]{1,0:T(8,128)(2,1)S(1)}, bf16[512,128]{1,0:T(8,128)(2,1)S(1)}) custom-call(bf16[2048,128]{1,0:T(8,128)(2,1)} %bitcast.15, bf16[2048,128]{1,0:T(8,128)(2,1)} %bitcast.16, bf16[512,128]{1,0:T(8,128)(2,1)} %bitcast.17, bf16[512,128]{1,0:T(8,128)(2,1)} %bitcast.18, s32[16,32]{1,0:T(8,128)} %bitcast.19, ...), custom_call_target="tpu_custom_call" | custom-call | tf_op jit(solution)/shard_map/pallas_call | solution.py:515
  28.8 0.9 %shard_map.86 = (bf16[2048,128]{1,0:T(8,128)(2,1)}, bf16[512,128]{1,0:T(8,128)(2,1)}, bf16[512,128]{1,0:T(8,128)(2,1)}) custom-call(bf16[2048,128]{1,0:T(8,128)(2,1)S(1)} %get-tuple-element.9.refs_0_, bf16[512,128]{1,0:T(8,128)(2,1)S(1)} %get-tuple-element.10.refs_1_, bf16[512,128]{1,0:T(8,128)(2,1)S(1)} %get-tuple-element.11.refs_2_), custom_call_target="tpu_custom_call" | custom-call | tf_op jit(solution)/shard_map/pallas_call | solution.py:484

commit v3 on v2

--- a/solution.py
+++ b/solution.py
@@ -39,12 +39,12 @@
     cfg,
     q_ref, do_ref, k_ref, v_ref, idx_hbm, val_hbm,
     dq_ref, dk_ref, dv_ref,
-    sel, qaug, qd, kv, oh, kt, stage, pool, wt,
-    s_own, dp_own, s_rem, dp_rem, pd, xsend, xrecv, tsend, trecv, ox_send, ox_recv, acc,
-    a_send, a_recv, f_send, f_recv, x_send, x_recv, t_send, t_recv, o_sem, r_sem, in_sem, stats,
-    ready, slots,
+    sel, qaug, qd, kv, oh, kt, vt, vt_own, dot_t, stage, pool, wt,
+    s_buf, pd, terms, xrecv, tsend, trecv, ox_send, ox_recv, acc,
+    a_send, a_recv, f_send, f_recv, x_send, x_recv, t_send, t_recv, o_sem, r_sem, in_sem,
+    ready, slots, st_m, st_l, st_d,
 ):
-    S, heads, nb, total, topk, width, supers, pre, nbuf = cfg
+    S, heads, nb, total, topk, width, pre = cfg
     me = lax.axis_index("seq")
     core = lax.axis_index("inner")
     mate = 1 - core
@@ -122,7 +122,7 @@
     def send_a(r):
         return pltpu.make_async_remote_copy(
             src_ref=stage.at[r],
-            dst_ref=pool.at[core, pl.ds(pl.multiple_of(me * chunk, chunk), chunk)],
+            dst_ref=pool.at[mate, pl.ds(pl.multiple_of(me * chunk, chunk), chunk)],
             send_sem=a_send.at[r],
             recv_sem=a_recv.at[me],
             device_id={"seq": r},
@@ -141,13 +141,19 @@
     loads[2].wait()
     loads[3].wait()
 
-    def give(j, _):
+    def choose(j, _):
         r = me + 1 + j
         code = code_of(r)
         across = dot(code, spread)[0:1, :].astype(jnp.int32) * BLK
         across = across + (iota((1, own_rows), 1) & (BLK - 1))
         pick = jnp.where(across == iota((chunk, own_rows), 0), 1.0, 0.0).astype(BF)
-        stage[r] = dot(pick, kv[core]).astype(BF)
+        stage[r] = dot(pick, kv[mate]).astype(BF)
+        return 0
+
+    lax.fori_loop(0, S - 1 - me, choose, 0)
+
+    def give(j, _):
+        r = me + 1 + j
         pl.semaphore_wait(ready.at[r], 1)
         send_a(r).start()
         return 0
@@ -185,22 +191,63 @@
     def own_count(b):
         return (b // pair + 1) * pair * BLK
 
-    def own_scores(b, at):
+    def fold(x, how):
+        return how(how(x.reshape(-1, 8, rows_b), axis=0), axis=0, keepdims=True)
+
+    def block_rows(b):
+        return pl.ds(b * rows_b, rows_b)
+
+    def soft(b, n, slot, keys_at):
+        s = s_buf[b, 0:n, :]
+        m = fold(s, jnp.max)
+        e = jnp.exp2((s - m) * c2)
+        st_m[slot, b : b + 1, :] = m
+        st_l[slot, b : b + 1, :] = fold(e, jnp.sum)
+        pd[1, keys_at, block_rows(b)] = e.astype(BF)
+
+    def lean(b, slot, turned_v, keys_at):
+        out = dot(turned_v, pd[1, keys_at, block_rows(b)])
+        st_d[slot, b : b + 1, :] = fold(out * dot_t[:, block_rows(b)], jnp.sum)
+
+    def grads(b, n, slot, vals, keys_at, delta):
+        rows = block_rows(b)
+        p = pd[1, keys_at, rows].astype(F32) * st_l[slot, b : b + 1, :]
+        dp = dot_nt(vals, qd[1, rows, :])
+        pd[1, keys_at, rows] = p.astype(BF)
+        pd[0, keys_at, rows] = (p * (dp - delta[b : b + 1, :])).astype(BF)
+
+    own_slot = S - 1
+    st_m[...] = jnp.full((S, nb, rows_b), NEG, F32)
+    st_l[...] = jnp.zeros((S, nb, rows_b), F32)
+    st_d[...] = jnp.zeros((S, nb, rows_b), F32)
+    vt_own[...] = kv[1].astype(F32).T.astype(BF)
+
+    def own_scores(b):
         n = own_count(b)
-        rows = pl.ds(b * rows_b, rows_b)
         ka = jnp.concatenate([kv[0, 0:n, :], oh[nrem : nrem + n, :]], axis=1)
-        s = dot_nt(ka, qaug[rows, :])
-        key = iota((n, rows_b), 0) - b * BLK
-        query = lax.shift_right_logical(iota((n, rows_b), 1), log2(heads))
-        s_own[at, 0:n, :] = jnp.where(key > query, NEG, s)
-        dp_own[at, 0:n, :] = dot_nt(kv[1, 0:n, :], qd[1, rows, :])
-
-    def fold(x, how):
-        return how(x.reshape(-1, 8, rows_b), axis=0)
-
-    if pre:
+        s = dot_nt(ka, qaug[block_rows(b), :])
+        lo, hi = b * BLK, (b + 1) * BLK
+        if lo:
+            s_buf[b, 0:lo, :] = s[0:lo]
+        key = iota((BLK, rows_b), 0)
+        query = lax.shift_right_logical(iota((BLK, rows_b), 1), log2(heads))
+        s_buf[b, lo:hi, :] = jnp.where(key > query, NEG, s[lo:hi])
+        if hi < n:
+            s_buf[b, hi:n, :] = s[hi:n]
+
+    def ahead(first, then):
+        first(0)
         for b in range(nb):
-            own_scores(b, b)
+            if b + 1 < nb:
+                first(b + 1)
+            then(b)
+
+    ahead(own_scores, lambda b: soft(b, own_count(b), own_slot, pl.ds(nrem, own_count(b))))
+    for b in range(nb):
+        rows = block_rows(b)
+        dot_t[:, rows] = qd[1, rows, :].astype(F32).T
+        n = own_count(b)
+        lean(b, own_slot, vt_own[:, 0:n], pl.ds(nrem, n))
 
     if pre:
 
@@ -215,6 +262,8 @@
         at = pl.ds(pl.multiple_of(s * chunk, chunk), chunk)
         pool[0, at, :] = jnp.zeros((chunk, width), BF)
         pool[1, at, :] = jnp.zeros((chunk, width), BF)
+        for b in range(nb):
+            pd[0, at, block_rows(b)] = jnp.zeros((chunk, rows_b), BF)
         return 0
 
     lax.fori_loop(me, S - 1, blank, 0)
@@ -225,7 +274,7 @@
     def recv_a(s):
         return pltpu.make_async_remote_copy(
             src_ref=stage.at[s],
-            dst_ref=pool_at(core, s),
+            dst_ref=pool_at(mate, s),
             send_sem=a_send.at[s],
             recv_sem=a_recv.at[s],
             device_id={"seq": s},
@@ -242,99 +291,59 @@
             device_id_type=MESH,
         )
 
-    def pass_on(j, _):
-        s = me - 1 - j
-        recv_a(s).wait_recv()
-        forward(core, s).start()
-        return 0
-
-    lax.fori_loop(0, me, pass_on, 0)
-
-    def take(j, _):
-        s = me - 1 - j
-        forward(mate, s).wait_recv()
-        return 0
-
-    lax.fori_loop(0, me, take, 0)
-
-    step = nrem // supers
-
-    def loop(body, init):
-        for j in range(supers):
-            init = body(j, init)
-        return init
-
-    def span(j):
-        return pl.ds(j * step, step)
-
-    for s in range(S - 1):
-        kt[:, s * chunk : (s + 1) * chunk] = (
-            pool[0, s * chunk : (s + 1) * chunk, :].astype(F32).T.astype(BF)
-        )
-
-    def third_on(s_view, dp_view, where, rows, keys_at, inv, delta):
-        p = s_view[where] * inv
-        pd[1, keys_at, rows] = p.astype(BF)
-        pd[0, keys_at, rows] = (p * (dp_view[where] - delta)).astype(BF)
-
-    for b in range(nb):
-        at = b if pre else 0
-        buf = b % nbuf
-        n = own_count(b)
-        rows = pl.ds(b * rows_b, rows_b)
-        if not pre:
-            own_scores(b, 0)
-        qa = qaug[rows, :]
-        dob = qd[1, rows, :]
-
-        def first(j, m):
-            here = span(j)
-            ka = jnp.concatenate([pool[0, here, :], oh[here, :]], axis=1)
-            s = dot_nt(ka, qa)
-            s_rem[buf, here, :] = s
-            dp_rem[buf, here, :] = dot_nt(pool[1, here, :], dob)
-            return jnp.maximum(m, fold(s, jnp.max))
-
-        m = loop(first, fold(s_own[at, 0:n, :], jnp.max))
-        m = jnp.max(m, axis=0, keepdims=True)
-
-        def second_on(s_view, dp_view, where, carry):
-            l, d = carry
-            e = jnp.exp2((s_view[where] - m) * c2)
-            s_view[where] = e
-            return (
-                l + fold(e, jnp.sum),
-                d + fold(e * dp_view[where], jnp.sum),
-            )
-
-        zero = jnp.zeros((8, rows_b), F32)
-        carry = second_on(s_own, dp_own, (at, slice(0, n)), (zero, zero))
-        l, d = loop(lambda j, c: second_on(s_rem, dp_rem, (buf, span(j)), c), carry)
-        inv = 1.0 / jnp.sum(l, axis=0, keepdims=True)
-        delta = jnp.sum(d, axis=0, keepdims=True) * inv
-
-        if pre:
-            stats[b, 0:1, :] = inv
-            stats[b, 1:2, :] = delta
-        else:
-            third_on(s_own, dp_own, (at, slice(0, n)), rows, pl.ds(nrem, n), inv, delta)
-
-        def third(j, c):
-            third_on(s_rem, dp_rem, (buf, span(j)), rows, span(j), inv, delta)
-            return c
-
-        loop(third, 0)
+    def keys_of(s):
+        return pl.ds(pl.multiple_of(s * chunk, chunk), chunk)
+
+    def partial(s):
+        at = keys_of(s)
+        vt[s] = pool[1, at, :].astype(F32).T.astype(BF)
+
+        def scores(b):
+            ka = jnp.concatenate([pool[0, at, :], oh[at, :]], axis=1)
+            s_buf[b, 0:chunk, :] = dot_nt(ka, qaug[block_rows(b), :])
+
+        ahead(scores, lambda b: soft(b, chunk, s, at))
+        for b in range(nb):
+            lean(b, s, vt[s], at)
+
+    def arrive(j, _):
+        @pl.when(j < me)
+        def _():
+            s = me - 1 - j
+            recv_a(s).wait_recv()
+            forward(mate, s).start()
+
+        @pl.when(j > 0)
+        def _():
+            s = me - j
+            forward(core, s).wait_recv()
+            partial(s)
+
+        return 0
+
+    lax.fori_loop(0, me + 1, arrive, 0)
+
+    top = st_m[0]
+    for s in range(1, S):
+        top = jnp.maximum(top, st_m[s])
+    mass = jnp.zeros((nb, rows_b), F32)
+    delta = jnp.zeros((nb, rows_b), F32)
+    for s in range(S):
+        w = jnp.exp2((st_m[s] - top) * c2)
+        st_m[s] = w
+        mass += w * st_l[s]
+        delta += w * st_d[s]
+    inv = 1.0 / mass
+    st_d[0] = delta * inv
+    for s in range(S):
+        st_l[s] = st_m[s] * inv
 
     def scale_of(kind):
         return jnp.where(kind == 0, scaling, 1.0).astype(F32)
 
-    def remote_terms(kind, s):
-        at = pl.ds(pl.multiple_of(s * chunk, chunk), chunk)
-        return dot(pd[kind, at, :], qd[kind]) * scale_of(kind)
-
     def swap(s):
         return pltpu.make_async_remote_copy(
-            src_ref=xsend.at[s],
+            src_ref=terms.at[s, mate],
             dst_ref=xrecv.at[s],
             send_sem=x_send.at[s],
             recv_sem=x_recv.at[s],
@@ -352,25 +361,31 @@
             device_id_type=MESH,
         )
 
-    def other(s, _):
-        xsend[s] = remote_terms(mate, s)
+    def finish(s):
+        swap(s).wait_recv()
+        tsend[s] = (terms[s, core] + xrecv[s]).astype(BF)
+        give_back(s).start()
+
+    def remote(s, _):
+        at = keys_of(s)
+        delta = st_d[0]
+        for b in range(nb):
+            grads(b, chunk, s, pool[1, at, :], at, delta)
+        terms[s, 1] = dot(pd[1, at, :], qd[1])
+        terms[s, 0] = dot(pd[0, at, :], qd[0]) * scaling
         swap(s).start()
-        return 0
-
-    lax.fori_loop(0, jnp.minimum(me, 1), other, 0)
-
-    def ours(s, _):
-        @pl.when(s + 1 < me)
+
+        @pl.when(s > 0)
         def _():
-            other(s + 1, 0)
-
-        total_terms = remote_terms(core, s)
-        swap(s).wait_recv()
-        tsend[s] = (total_terms + xrecv[s]).astype(BF)
-        give_back(s).start()
-        return 0
-
-    lax.fori_loop(0, me, ours, 0)
+            finish(s - 1)
+
+        return 0
+
+    lax.fori_loop(0, me, remote, 0)
+
+    @pl.when(me > 0)
+    def _():
+        finish(me - 1)
 
     own_swap = pltpu.make_async_remote_copy(
         src_ref=ox_send,
@@ -390,17 +405,18 @@
                 * scale_of(kind)
             )
 
-    if pre:
-        for b in range(nb):
-            n = own_count(b)
-            third_on(
-                s_own, dp_own, (b, slice(0, n)), pl.ds(b * rows_b, rows_b), pl.ds(nrem, n),
-                stats[b, 0:1, :], stats[b, 1:2, :],
-            )
+    delta = st_d[0]
+    for b in range(nb):
+        n = own_count(b)
+        grads(b, n, own_slot, kv[1, 0:n, :], pl.ds(nrem, n), delta)
     own_terms(mate, ox_send)
     own_swap.start()
     own_terms(core, acc)
 
+    for s in range(S - 1):
+        kt[:, s * chunk : (s + 1) * chunk] = (
+            pool[0, s * chunk : (s + 1) * chunk, :].astype(F32).T.astype(BF)
+        )
     for b in range(nb):
         rows = pl.ds(b * rows_b, rows_b)
         n = nrem + own_count(b)
@@ -452,7 +468,7 @@
     lax.fori_loop(0, S - 1 - me, close_up, 0)
 
     def close_down(s, _):
-        forward(core, s).wait_send()
+        forward(mate, s).wait_send()
         swap(s).wait_send()
         give_back(s).wait_send()
         return 0
@@ -504,11 +520,8 @@
     rows_b = BLK * heads
     lanes = -(-total // 128) * 128
     slot_lanes = -(-(nkeys // BLK) // 128) * 128
-    supers = next(n for n in range(1, S) if (S - 1) % n == 0 and (S - 1) // n <= 4)
-    pre = supers == 1
-    nbuf = 2 if pre else 1
-    n_own = nb if pre else 1
-    cfg = (S, heads, nb, total, topk, width, supers, pre, nbuf)
+    pre = S <= 4
+    cfg = (S, heads, nb, total, topk, width, pre)
     vmem = pl.BlockSpec(memory_space=pltpu.VMEM)
     hbm = pl.BlockSpec(memory_space=pl.ANY)
     dma = pltpu.SemaphoreType.DMA
@@ -528,15 +541,15 @@
             pltpu.VMEM((2, own_rows, width), BF),
             pltpu.VMEM((nkeys, slot_lanes), BF),
             pltpu.VMEM((width, nkeys), BF),
+            pltpu.VMEM((S - 1, width, chunk), BF),
+            pltpu.VMEM((width, own_rows), BF),
+            pltpu.VMEM((width, rows), F32),
             pltpu.VMEM((S, chunk, width), BF),
             pltpu.VMEM((2, nrem, width), BF),
             pltpu.VMEM((S if pre else 1, own_rows, chunk), BF),
-            pltpu.VMEM((n_own, own_rows, rows_b), F32),
-            pltpu.VMEM((n_own, own_rows, rows_b), F32),
-            pltpu.VMEM((nbuf, nrem, rows_b), F32),
-            pltpu.VMEM((nbuf, nrem, rows_b), F32),
+            pltpu.VMEM((nb, max(own_rows, chunk), rows_b), F32),
             pltpu.VMEM((2, nkeys, rows), BF),
-            pltpu.VMEM((S, chunk, width), F32),
+            pltpu.VMEM((S, 2, chunk, width), F32),
             pltpu.VMEM((S, chunk, width), F32),
             pltpu.VMEM((S, chunk, width), BF),
             pltpu.VMEM((S, chunk, width), BF),
@@ -546,9 +559,11 @@
             dma((S,)), dma((S,)), dma((S,)), dma((S,)), dma((S,)), dma((S,)),
             dma((S,)), dma((S,)), dma((2,)), dma((2,)),
             dma((6,)),
-            pltpu.VMEM((nb, 2, rows_b), F32),
             pltpu.SemaphoreType.REGULAR((S,)),
             pltpu.VMEM((2, topk, total), jnp.int32),
+            pltpu.VMEM((S, nb, rows_b), F32),
+            pltpu.VMEM((S, nb, rows_b), F32),
+            pltpu.VMEM((S, nb, rows_b), F32),
         ],
         compiler_params=pltpu.CompilerParams(
             collective_id=0, has_side_effects=True, vmem_limit_bytes=67043328 - 6 * own_rows * width * 2 - 4096

time: 29.9 us -> 26.7 us (0.89)
  Pallas kernels: 29.1 us -> 25.8 us
    pallas_call x1, Pallas kernels: 28.2 us -> 24.9 us  [per_device(): pl.pallas_call(functools.partial(kernel, cfg), out_shape=(pltpu.VMEM((row...]
where the time goes in v3:
time: 26.7 us; the launch traced here: 26.5 us
  Pallas kernels  25.8 us (97%)
  between operations  0.64 us (2%)
    pallas_call x1, Pallas kernels, per_device(): pl.pallas_call(functools.partial(kernel, cfg), out_shape=(pltpu.VMEM((row...  24.9 us
    pallas_call x1, Pallas kernels, place(): pl.pallas_call(place_kernel, out_shape=tuple((jax.ShapeDtypeStruct(a.shap...  0.9 us

profile of v3, /device:TPU:0, one launch (start us, length us, event | category | flops | bytes accessed | tf_op | source)
XLA Modules:
  0.0 26.5 jit_solution(15794293218997662676)
XLA Ops:
  0.6 24.9 %shard_map.85 = (bf16[2048,128]{1,0:T(8,128)(2,1)S(1)}, bf16[512,128]{1,0:T(8,128)(2,1)S(1)}, bf16[512,128]{1,0:T(8,128)(2,1)S(1)}) custom-call(bf16[2048,128]{1,0:T(8,128)(2,1)} %bitcast.15, bf16[2048,128]{1,0:T(8,128)(2,1)} %bitcast.16, bf16[512,128]{1,0:T(8,128)(2,1)} %bitcast.17, bf16[512,128]{1,0:T(8,128)(2,1)} %bitcast.18, s32[16,32]{1,0:T(8,128)} %bitcast.19, ...), custom_call_target="tpu_custom_call" | custom-call | tf_op jit(solution)/shard_map/pallas_call | solution.py:528
  25.6 0.9 %shard_map.86 = (bf16[2048,128]{1,0:T(8,128)(2,1)}, bf16[512,128]{1,0:T(8,128)(2,1)}, bf16[512,128]{1,0:T(8,128)(2,1)}) custom-call(bf16[2048,128]{1,0:T(8,128)(2,1)S(1)} %get-tuple-element.9.refs_0_, bf16[512,128]{1,0:T(8,128)(2,1)S(1)} %get-tuple-element.10.refs_1_, bf16[512,128]{1,0:T(8,128)(2,1)S(1)} %get-tuple-element.11.refs_2_), custom_call_target="tpu_custom_call" | custom-call | tf_op jit(solution)/shard_map/pallas_call | solution.py:500

commit v4 on v3

--- a/solution.py
+++ b/solution.py
@@ -39,7 +39,7 @@
     cfg,
     q_ref, do_ref, k_ref, v_ref, idx_hbm, val_hbm,
     dq_ref, dk_ref, dv_ref,
-    sel, qaug, qd, kv, oh, kt, vt, vt_own, dot_t, stage, pool, wt,
+    sel, qaug, qd, kv, oh, kt, vt_own, dot_t, stage, pool, wt,
     s_buf, pd, terms, xrecv, tsend, trecv, ox_send, ox_recv, acc,
     a_send, a_recv, f_send, f_recv, x_send, x_recv, t_send, t_recv, o_sem, r_sem, in_sem,
     ready, slots, st_m, st_l, st_d,
@@ -198,10 +198,7 @@
         return pl.ds(b * rows_b, rows_b)
 
     def soft(b, n, slot, keys_at):
-        s = s_buf[b, 0:n, :]
-        m = fold(s, jnp.max)
-        e = jnp.exp2((s - m) * c2)
-        st_m[slot, b : b + 1, :] = m
+        e = jnp.exp2((s_buf[b, 0:n, :] - st_m[slot, b : b + 1, :]) * c2)
         st_l[slot, b : b + 1, :] = fold(e, jnp.sum)
         pd[1, keys_at, block_rows(b)] = e.astype(BF)
 
@@ -227,13 +224,16 @@
         ka = jnp.concatenate([kv[0, 0:n, :], oh[nrem : nrem + n, :]], axis=1)
         s = dot_nt(ka, qaug[block_rows(b), :])
         lo, hi = b * BLK, (b + 1) * BLK
-        if lo:
-            s_buf[b, 0:lo, :] = s[0:lo]
         key = iota((BLK, rows_b), 0)
         query = lax.shift_right_logical(iota((BLK, rows_b), 1), log2(heads))
-        s_buf[b, lo:hi, :] = jnp.where(key > query, NEG, s[lo:hi])
+        parts = [jnp.where(key > query, NEG, s[lo:hi])]
+        if lo:
+            parts.insert(0, s[0:lo])
         if hi < n:
-            s_buf[b, hi:n, :] = s[hi:n]
+            parts.append(s[hi:n])
+        s = jnp.concatenate(parts, axis=0)
+        s_buf[b, 0:n, :] = s
+        st_m[own_slot, b : b + 1, :] = fold(s, jnp.max)
 
     def ahead(first, then):
         first(0)
@@ -294,34 +294,62 @@
     def keys_of(s):
         return pl.ds(pl.multiple_of(s * chunk, chunk), chunk)
 
-    def partial(s):
+    def weigh(s):
         at = keys_of(s)
-        vt[s] = pool[1, at, :].astype(F32).T.astype(BF)
 
         def scores(b):
             ka = jnp.concatenate([pool[0, at, :], oh[at, :]], axis=1)
-            s_buf[b, 0:chunk, :] = dot_nt(ka, qaug[block_rows(b), :])
+            part = dot_nt(ka, qaug[block_rows(b), :])
+            s_buf[b, 0:chunk, :] = part
+            st_m[s, b : b + 1, :] = fold(part, jnp.max)
 
         ahead(scores, lambda b: soft(b, chunk, s, at))
+
+    def average(s):
+        at = keys_of(s)
+        turned_v = pool[1, at, :].astype(F32).T.astype(BF)
         for b in range(nb):
-            lean(b, s, vt[s], at)
-
-    def arrive(j, _):
-        @pl.when(j < me)
+            lean(b, s, turned_v, at)
+
+    def land(s):
+        recv_a(s).wait_recv()
+        forward(mate, s).start()
+
+    def keys_in(s):
+        @pl.when(core == 1)
         def _():
-            s = me - 1 - j
-            recv_a(s).wait_recv()
-            forward(mate, s).start()
-
-        @pl.when(j > 0)
+            land(s)
+
+        @pl.when(core == 0)
         def _():
-            s = me - j
             forward(core, s).wait_recv()
-            partial(s)
-
-        return 0
-
-    lax.fori_loop(0, me + 1, arrive, 0)
+
+        weigh(s)
+
+    def values_in(s):
+        @pl.when(core == 1)
+        def _():
+            forward(core, s).wait_recv()
+
+        average(s)
+
+    def down(first, body):
+        def at(j, _):
+            body(me - 1 - j)
+            return 0
+
+        lax.fori_loop(first, me, at, 0)
+
+    @pl.when(me > 0)
+    def _():
+        keys_in(me - 1)
+
+    @pl.when(core == 0)
+    def _():
+        down(0, land)
+
+    down(1, keys_in)
+    down(0, values_in)
 
     top = st_m[0]
     for s in range(1, S):
@@ -541,7 +569,6 @@
             pltpu.VMEM((2, own_rows, width), BF),
             pltpu.VMEM((nkeys, slot_lanes), BF),
             pltpu.VMEM((width, nkeys), BF),
-            pltpu.VMEM((S - 1, width, chunk), BF),
             pltpu.VMEM((width, own_rows), BF),
             pltpu.VMEM((width, rows), F32),
             pltpu.VMEM((S, chunk, width), BF),

time: 26.7 us -> 25.4 us (0.951)
  Pallas kernels: 25.8 us -> 24.5 us
    pallas_call x1, Pallas kernels: 24.9 us -> 23.6 us  [per_device(): pl.pallas_call(functools.partial(kernel, cfg), out_shape=(pltpu.VMEM((row...]
where the time goes in v4:
time: 25.4 us; the launch traced here: 25.1 us
  Pallas kernels  24.5 us (96%)
  between operations  0.64 us (3%)
    pallas_call x1, Pallas kernels, per_device(): pl.pallas_call(functools.partial(kernel, cfg), out_shape=(pltpu.VMEM((row...  23.6 us
    pallas_call x1, Pallas kernels, place(): pl.pallas_call(place_kernel, out_shape=tuple((jax.ShapeDtypeStruct(a.shap...  0.9 us

profile of v4, /device:TPU:0, one launch (start us, length us, event | category | flops | bytes accessed | tf_op | source)
XLA Modules:
  0.0 25.1 jit_solution(3898867587448659515)
XLA Ops:
  0.6 23.6 %shard_map.85 = (bf16[2048,128]{1,0:T(8,128)(2,1)S(1)}, bf16[512,128]{1,0:T(8,128)(2,1)S(1)}, bf16[512,128]{1,0:T(8,128)(2,1)S(1)}) custom-call(bf16[2048,128]{1,0:T(8,128)(2,1)} %bitcast.15, bf16[2048,128]{1,0:T(8,128)(2,1)} %bitcast.16, bf16[512,128]{1,0:T(8,128)(2,1)} %bitcast.17, bf16[512,128]{1,0:T(8,128)(2,1)} %bitcast.18, s32[16,32]{1,0:T(8,128)} %bitcast.19, ...), custom_call_target="tpu_custom_call" | custom-call | tf_op jit(solution)/shard_map/pallas_call | solution.py:556
  24.2 0.9 %shard_map.86 = (bf16[2048,128]{1,0:T(8,128)(2,1)}, bf16[512,128]{1,0:T(8,128)(2,1)}, bf16[512,128]{1,0:T(8,128)(2,1)}) custom-call(bf16[2048,128]{1,0:T(8,128)(2,1)S(1)} %get-tuple-element.9.refs_0_, bf16[512,128]{1,0:T(8,128)(2,1)S(1)} %get-tuple-element.10.refs_1_, bf16[512,128]{1,0:T(8,128)(2,1)S(1)} %get-tuple-element.11.refs_2_), custom_call_target="tpu_custom_call" | custom-call | tf_op jit(solution)/shard_map/pallas_call | solution.py:528

commit v5 on v4

--- a/solution.py
+++ b/solution.py
@@ -40,7 +40,7 @@
     q_ref, do_ref, k_ref, v_ref, idx_hbm, val_hbm,
     dq_ref, dk_ref, dv_ref,
     sel, qaug, qd, kv, oh, kt, vt_own, dot_t, stage, pool, wt,
-    s_buf, pd, terms, xrecv, tsend, trecv, ox_send, ox_recv, acc,
+    s_buf, pd, p_run, terms, xrecv, tsend, trecv, ox_send, ox_recv, acc,
     a_send, a_recv, f_send, f_recv, x_send, x_recv, t_send, t_recv, o_sem, r_sem, in_sem,
     ready, slots, st_m, st_l, st_d,
 ):
@@ -64,6 +64,12 @@
         return 0
 
     lax.fori_loop(0, S - 1 - me, hello, 0)
+    middle = S // 2
+
+    @pl.when(me == middle)
+    def _():
+        pl.semaphore_signal(barrier, inc=1, device_id={"seq": middle - 1}, device_id_type=MESH)
+
     pl.semaphore_signal(barrier, inc=1, device_id={"inner": mate}, device_id_type=MESH)
 
     loads = [
@@ -78,13 +84,16 @@
     for load in loads:
         load.start()
 
-    pl.semaphore_wait(barrier, me + 1)
+    waits = me == middle - 1
 
     def answer(j, _):
         pl.semaphore_signal(ready.at[me], inc=1, device_id={"seq": j}, device_id_type=MESH)
         return 0
 
-    lax.fori_loop(0, me, answer, 0)
+    @pl.when(jnp.logical_not(waits))
+    def _():
+        pl.semaphore_wait(barrier, me + 1)
+        lax.fori_loop(0, jnp.where(me == middle, me - 1, me), answer, 0)
 
     loads[0].wait()
     loads[1].wait()
@@ -143,6 +152,13 @@
 
     def choose(j, _):
         r = me + 1 + j
+
+        @pl.when(waits & (j == 1))
+        def _():
+            pl.semaphore_wait(barrier, me + 2)
+            lax.fori_loop(0, me, answer, 0)
+            send_a(r - 1).start()
+
         code = code_of(r)
         across = dot(code, spread)[0:1, :].astype(jnp.int32) * BLK
         across = across + (iota((1, own_rows), 1) & (BLK - 1))
@@ -158,7 +174,7 @@
         send_a(r).start()
         return 0
 
-    lax.fori_loop(0, S - 1 - me, give, 0)
+    lax.fori_loop(jnp.where(waits, 1, 0), S - 1 - me, give, 0)
 
     mine, present, rank = ranks(me)
     block_row = iota((1, lanes), 1)
@@ -206,11 +222,12 @@
         out = dot(turned_v, pd[1, keys_at, block_rows(b)])
         st_d[slot, b : b + 1, :] = fold(out * dot_t[:, block_rows(b)], jnp.sum)
 
-    def grads(b, n, slot, vals, keys_at, delta):
+    def probs(b, slot, keys_at):
+        return pd[1, keys_at, block_rows(b)].astype(F32) * st_l[slot, b : b + 1, :]
+
+    def grads(b, p, vals, keys_at, delta):
         rows = block_rows(b)
-        p = pd[1, keys_at, rows].astype(F32) * st_l[slot, b : b + 1, :]
         dp = dot_nt(vals, qd[1, rows, :])
-        pd[1, keys_at, rows] = p.astype(BF)
         pd[0, keys_at, rows] = (p * (dp - delta[b : b + 1, :])).astype(BF)
 
     own_slot = S - 1
@@ -344,12 +361,22 @@
     def _():
         keys_in(me - 1)
 
+    early = jnp.where(me == S - 1, 1, 0)
+
+    @pl.when(early == 1)
+    def _():
+        @pl.when(core == 0)
+        def _():
+            land(me - 1)
+
+        values_in(me - 1)
+
     @pl.when(core == 0)
     def _():
-        down(0, land)
+        down(early, land)
 
     down(1, keys_in)
-    down(0, values_in)
+    down(early, values_in)
 
     top = st_m[0]
     for s in range(1, S):
@@ -398,14 +425,24 @@
         at = keys_of(s)
         delta = st_d[0]
         for b in range(nb):
-            grads(b, chunk, s, pool[1, at, :], at, delta)
-        terms[s, 1] = dot(pd[1, at, :], qd[1])
+            p_run[:, block_rows(b)] = probs(b, s, at).astype(BF)
+        terms[s, 1] = dot(p_run[...], qd[1])
+
+        @pl.when(core == 0)
+        def _():
+            swap(s).start()
+
+        @pl.when(s > 0)
+        def _():
+            finish(s - 1)
+
+        for b in range(nb):
+            grads(b, probs(b, s, at), pool[1, at, :], at, delta)
         terms[s, 0] = dot(pd[0, at, :], qd[0]) * scaling
-        swap(s).start()
-
-        @pl.when(s > 0)
-        def _():
-            finish(s - 1)
+
+        @pl.when(core == 1)
+        def _():
+            swap(s).start()
 
         return 0
 
@@ -436,7 +473,9 @@
     delta = st_d[0]
     for b in range(nb):
         n = own_count(b)
-        grads(b, n, own_slot, kv[1, 0:n, :], pl.ds(nrem, n), delta)
+        p = probs(b, own_slot, pl.ds(nrem, n))
+        pd[1, pl.ds(nrem, n), block_rows(b)] = p.astype(BF)
+        grads(b, p, kv[1, 0:n, :], pl.ds(nrem, n), delta)
     own_terms(mate, ox_send)
     own_swap.start()
     own_terms(core, acc)
@@ -576,6 +615,7 @@
             pltpu.VMEM((S if pre else 1, own_rows, chunk), BF),
             pltpu.VMEM((nb, max(own_rows, chunk), rows_b), F32),
             pltpu.VMEM((2, nkeys, rows), BF),
+            pltpu.VMEM((chunk, rows), BF),
             pltpu.VMEM((S, 2, chunk, width), F32),
             pltpu.VMEM((S, chunk, width), F32),
             pltpu.VMEM((S, chunk, width), BF),

time: 25.4 us -> 24.2 us (0.953)
  Pallas kernels: 24.5 us -> 23.2 us
    pallas_call x1, Pallas kernels: 23.6 us -> 22.3 us  [per_device(): pl.pallas_call(functools.partial(kernel, cfg), out_shape=(pltpu.VMEM((row...]
where the time goes in v5:
time: 24.2 us; the launch traced here: 23.9 us
  Pallas kernels  23.2 us (96%)
  between operations  0.64 us (3%)
    pallas_call x1, Pallas kernels, per_device(): pl.pallas_call(functools.partial(kernel, cfg), out_shape=(pltpu.VMEM((row...  22.3 us
    pallas_call x1, Pallas kernels, place(): pl.pallas_call(place_kernel, out_shape=tuple((jax.ShapeDtypeStruct(a.shap...  0.9 us

profile of v5, /device:TPU:0, one launch (start us, length us, event | category | flops | bytes accessed | tf_op | source)
XLA Modules:
  0.0 23.9 jit_solution(17227565485486199330)
XLA Ops:
  0.6 22.3 %shard_map.85 = (bf16[2048,128]{1,0:T(8,128)(2,1)S(1)}, bf16[512,128]{1,0:T(8,128)(2,1)S(1)}, bf16[512,128]{1,0:T(8,128)(2,1)S(1)}) custom-call(bf16[2048,128]{1,0:T(8,128)(2,1)} %bitcast.15, bf16[2048,128]{1,0:T(8,128)(2,1)} %bitcast.16, bf16[512,128]{1,0:T(8,128)(2,1)} %bitcast.17, bf16[512,128]{1,0:T(8,128)(2,1)} %bitcast.18, s32[16,32]{1,0:T(8,128)} %bitcast.19, ...), custom_call_target="tpu_custom_call" | custom-call | tf_op jit(solution)/shard_map/pallas_call | solution.py:595
  23.0 0.9 %shard_map.86 = (bf16[2048,128]{1,0:T(8,128)(2,1)}, bf16[512,128]{1,0:T(8,128)(2,1)}, bf16[512,128]{1,0:T(8,128)(2,1)}) custom-call(bf16[2048,128]{1,0:T(8,128)(2,1)S(1)} %get-tuple-element.9.refs_0_, bf16[512,128]{1,0:T(8,128)(2,1)S(1)} %get-tuple-element.10.refs_1_, bf16[512,128]{1,0:T(8,128)(2,1)S(1)} %get-tuple-element.11.refs_2_), custom_call_target="tpu_custom_call" | custom-call | tf_op jit(solution)/shard_map/pallas_call | solution.py:567

commit v6 on v5

--- a/solution.py
+++ b/solution.py
@@ -39,7 +39,7 @@
     cfg,
     q_ref, do_ref, k_ref, v_ref, idx_hbm, val_hbm,
     dq_ref, dk_ref, dv_ref,
-    sel, qaug, qd, kv, oh, kt, vt_own, dot_t, stage, pool, wt,
+    sel, qaug, qd, kv, oh, kt, vt, vt_own, dot_t, do_t, stage, pool, wt,
     s_buf, pd, p_run, terms, xrecv, tsend, trecv, ox_send, ox_recv, acc,
     a_send, a_recv, f_send, f_recv, x_send, x_recv, t_send, t_recv, o_sem, r_sem, in_sem,
     ready, slots, st_m, st_l, st_d,
@@ -186,13 +186,13 @@
     )
     place = jnp.where((present > 0.5) & (run_row <= me), place, -1)
     table = jnp.where(place == iota((slot_lanes, lanes), 0), 1.0, 0.0).astype(BF)
-    bias = jnp.where(dot_nt(mine.astype(BF), table) > 0.5, 0.0, NEG)
+    bias = jnp.where(dot_nt(table, mine.astype(BF)) > 0.5, 0.0, NEG)
     loads[4].wait()
     loads[5].wait()
     for b in range(nb):
         rows = pl.ds(b * rows_b, rows_b)
-        qaug[rows, 0:width] = qd[0, rows, :]
-        qaug[rows, width:] = jnp.broadcast_to(bias[b : b + 1, :], (rows_b, slot_lanes)).astype(BF)
+        qaug[0:width, rows] = qd[0, rows, :].astype(F32).T.astype(BF)
+        qaug[width:, rows] = jnp.broadcast_to(bias[:, b : b + 1], (slot_lanes, rows_b)).astype(BF)
     nkeys = oh.shape[0]
     oh[...] = jnp.where(
         lax.shift_right_logical(iota((nkeys, slot_lanes), 0), log2(BLK))
@@ -215,19 +215,20 @@
 
     def soft(b, n, slot, keys_at):
         e = jnp.exp2((s_buf[b, 0:n, :] - st_m[slot, b : b + 1, :]) * c2)
-        st_l[slot, b : b + 1, :] = fold(e, jnp.sum)
         pd[1, keys_at, block_rows(b)] = e.astype(BF)
 
     def lean(b, slot, turned_v, keys_at):
-        out = dot(turned_v, pd[1, keys_at, block_rows(b)])
-        st_d[slot, b : b + 1, :] = fold(out * dot_t[:, block_rows(b)], jnp.sum)
+        ones = jnp.ones((16, turned_v.shape[1]), BF)
+        out = dot(jnp.concatenate([turned_v, ones], axis=0), pd[1, keys_at, block_rows(b)])
+        st_l[slot, b : b + 1, :] = out[width : width + 1]
+        st_d[slot, b : b + 1, :] = fold(out[0:width] * dot_t[:, block_rows(b)], jnp.sum)
 
     def probs(b, slot, keys_at):
         return pd[1, keys_at, block_rows(b)].astype(F32) * st_l[slot, b : b + 1, :]
 
     def grads(b, p, vals, keys_at, delta):
         rows = block_rows(b)
-        dp = dot_nt(vals, qd[1, rows, :])
+        dp = dot(vals, do_t[:, rows])
         pd[0, keys_at, rows] = (p * (dp - delta[b : b + 1, :])).astype(BF)
 
     own_slot = S - 1
@@ -239,7 +240,7 @@
     def own_scores(b):
         n = own_count(b)
         ka = jnp.concatenate([kv[0, 0:n, :], oh[nrem : nrem + n, :]], axis=1)
-        s = dot_nt(ka, qaug[block_rows(b), :])
+        s = dot(ka, qaug[:, block_rows(b)])
         lo, hi = b * BLK, (b + 1) * BLK
         key = iota((BLK, rows_b), 0)
         query = lax.shift_right_logical(iota((BLK, rows_b), 1), log2(heads))
@@ -262,7 +263,9 @@
     ahead(own_scores, lambda b: soft(b, own_count(b), own_slot, pl.ds(nrem, own_count(b))))
     for b in range(nb):
         rows = block_rows(b)
-        dot_t[:, rows] = qd[1, rows, :].astype(F32).T
+        turned_do = qd[1, rows, :].astype(F32).T
+        dot_t[:, rows] = turned_do
+        do_t[:, rows] = turned_do.astype(BF)
         n = own_count(b)
         lean(b, own_slot, vt_own[:, 0:n], pl.ds(nrem, n))
 
@@ -316,7 +319,7 @@
 
         def scores(b):
             ka = jnp.concatenate([pool[0, at, :], oh[at, :]], axis=1)
-            part = dot_nt(ka, qaug[block_rows(b), :])
+            part = dot(ka, qaug[:, block_rows(b)])
             s_buf[b, 0:chunk, :] = part
             st_m[s, b : b + 1, :] = fold(part, jnp.max)
 
@@ -324,14 +327,20 @@
 
     def average(s):
         at = keys_of(s)
-        turned_v = pool[1, at, :].astype(F32).T.astype(BF)
         for b in range(nb):
-            lean(b, s, turned_v, at)
+            lean(b, s, vt[s], at)
+
+    def turn(s):
+        vt[s] = pool[1, keys_of(s), :].astype(F32).T.astype(BF)
 
     def land(s):
         recv_a(s).wait_recv()
         forward(mate, s).start()
 
+    def land_values(s):
+        land(s)
+        turn(s)
+
     def keys_in(s):
         @pl.when(core == 1)
         def _():
@@ -347,6 +356,7 @@
         @pl.when(core == 1)
         def _():
             forward(core, s).wait_recv()
+            turn(s)
 
         average(s)
 
@@ -367,13 +377,13 @@
     def _():
         @pl.when(core == 0)
         def _():
-            land(me - 1)
+            land_values(me - 1)
 
         values_in(me - 1)
 
     @pl.when(core == 0)
     def _():
-        down(early, land)
+        down(early, land_values)
 
     down(1, keys_in)
     down(early, values_in)
@@ -603,13 +613,15 @@
         out_specs=(vmem, vmem, vmem),
         scratch_shapes=[
             pltpu.VMEM((total, lanes), F32),
-            pltpu.VMEM((rows, width + slot_lanes), BF),
+            pltpu.VMEM((width + slot_lanes, rows), BF),
             pltpu.VMEM((2, rows, width), BF),
             pltpu.VMEM((2, own_rows, width), BF),
             pltpu.VMEM((nkeys, slot_lanes), BF),
             pltpu.VMEM((width, nkeys), BF),
+            pltpu.VMEM((S - 1, width, chunk), BF),
             pltpu.VMEM((width, own_rows), BF),
             pltpu.VMEM((width, rows), F32),
+            pltpu.VMEM((width, rows), BF),
             pltpu.VMEM((S, chunk, width), BF),
             pltpu.VMEM((2, nrem, width), BF),
             pltpu.VMEM((S if pre else 1, own_rows, chunk), BF),

time: 24.2 us -> 23.9 us (0.988)
  no operation moved by 1% of the time
where the time goes in v6:
time: 23.9 us; the launch traced here: 23.7 us
  Pallas kernels  23 us (96%)
  between operations  0.64 us (3%)
    pallas_call x1, Pallas kernels, per_device(): pl.pallas_call(functools.partial(kernel, cfg), out_shape=(pltpu.VMEM((row...  22.1 us
    pallas_call x1, Pallas kernels, place(): pl.pallas_call(place_kernel, out_shape=tuple((jax.ShapeDtypeStruct(a.shap...  0.9 us

profile of v6, /device:TPU:0, one launch (start us, length us, event | category | flops | bytes accessed | tf_op | source)
XLA Modules:
  0.0 23.7 jit_solution(3047855246215284441)
XLA Ops:
  0.6 22.1 %shard_map.85 = (bf16[2048,128]{1,0:T(8,128)(2,1)S(1)}, bf16[512,128]{1,0:T(8,128)(2,1)S(1)}, bf16[512,128]{1,0:T(8,128)(2,1)S(1)}) custom-call(bf16[2048,128]{1,0:T(8,128)(2,1)} %bitcast.15, bf16[2048,128]{1,0:T(8,128)(2,1)} %bitcast.16, bf16[512,128]{1,0:T(8,128)(2,1)} %bitcast.17, bf16[512,128]{1,0:T(8,128)(2,1)} %bitcast.18, s32[16,32]{1,0:T(8,128)} %bitcast.19, ...), custom_call_target="tpu_custom_call" | custom-call | tf_op jit(solution)/shard_map/pallas_call | solution.py:605
  22.8 0.9 %shard_map.86 = (bf16[2048,128]{1,0:T(8,128)(2,1)}, bf16[512,128]{1,0:T(8,128)(2,1)}, bf16[512,128]{1,0:T(8,128)(2,1)}) custom-call(bf16[2048,128]{1,0:T(8,128)(2,1)S(1)} %get-tuple-element.9.refs_0_, bf16[512,128]{1,0:T(8,128)(2,1)S(1)} %get-tuple-element.10.refs_1_, bf16[512,128]{1,0:T(8,128)(2,1)S(1)} %get-tuple-element.11.refs_2_), custom_call_target="tpu_custom_call" | custom-call | tf_op jit(solution)/shard_map/pallas_call | solution.py:577
